TPU v7x, 512 devices: a 4x2x32 block of a 4x8x32 slice. The times are simulated.
512 devices in a mesh: real: 2 (over y), env: 32 (over z), mpo: 4 (over x), col: 2 (over core).
Axes of the slice: x: 4, y: 2, z: 32, core: 2. Of those that a mesh axis runs over, the one named last changes fastest.
The devices are a block of a 4x8x32 slice.
Arguments:
- held: bfloat16 [24576, 8, 384], P(('real', 'env', 'col')), parts along dimension 0, may hold values from -0.15625 to 0.15625
- owner_map: int32 [64, 192], P('real'), parts along dimension 0, may hold values from 0 to 12287, as said below
- kept: int32 [64], P(('real', 'env')), parts along dimension 0, may hold values from 96 to 384
- left_env: bfloat16 [16, 64, 384, 384], P('mpo', ('real', 'env')), parts along dimension 1, may hold values from -6 to 6
- mpo_tensor: float32 [14, 14, 4, 4], replicated, may hold values from -1 to 1
- mpo_mask: int32 [14, 14], replicated, may hold values 0 or 1
- fields: float32 [4], P('real'), parts along dimension 0, may hold values from -2 to 2
Outputs:
- new_env: float32 [16, 64, 384, 384], P('mpo', ('real', 'env'), None, 'col'), parts along dimension 1
There are 2 independent parts, one for each index of `real`. A program takes and returns all parts, laid end to end along the dimension named above; an argument that names none is the same for every part. Nothing has to cross between parts.
Inputs may be any that keep to these rules, and one draw needn't show every extreme that they name: owner_map[t, j] is the slot of held that holds tile j of sector t; all entries differ. The owner of index o along env+col holds the slots o * 192 to (o + 1) * 192 - 1. Among the tiles of one sector (the sector of one env index), one owner holds at most 6, and for every sector some owner holds exactly 6.
All inputs are finite; a program needn't handle non-finite values.
Results may differ from a plain program's by a relative error of at most 0.0042.
Values may be sent and summed in bfloat16 or wider, within the bound.
A program may use at most 64 MiB of HBM per device.

v0:
```python
import jax
import jax.numpy as jnp
from jax import lax
from jax.sharding import PartitionSpec as P


def in_order(tiles, dim):
    tiles = jnp.moveaxis(tiles, 0, dim)
    lengths = tiles.shape
    return tiles.reshape(*lengths[:dim], lengths[dim] * lengths[dim + 1], *lengths[dim + 2 :])


def sent_to_all(shard, axis):
    copies = jnp.broadcast_to(shard, (lax.axis_size(axis), *shard.shape))
    return lax.all_to_all(copies, axis, split_axis=0, concat_axis=0, tiled=True)


def collect(shard, axis, dim):
    return in_order(sent_to_all(shard, axis), dim)


def split_up(shard, dim, count):
    before, after = (shard.shape[:dim], shard.shape[dim + 1 :])
    return jnp.moveaxis(shard.reshape(*before, count, -1, *after), dim, 0)


def summed_on_arrival(shard, axis, dim):
    count = lax.axis_size(axis)
    tiles = lax.all_to_all(split_up(shard, dim, count), axis, 0, 0, tiled=True)
    return jnp.sum(tiles.astype(jnp.float32), axis=0)


def build_couplings(mpo_tensor, mpo_mask, fields, padded):
    bond = mpo_tensor.shape[0]
    states = mpo_tensor.shape[2]
    base = mpo_tensor * mpo_mask.astype(jnp.float32)[:, :, None, None]
    level = jnp.arange(states, dtype=jnp.int32)
    spin_first = 0.5 - (level // 2).astype(jnp.float32)
    spin_second = 0.5 - (level % 2).astype(jnp.float32)
    onsite = jnp.diag(fields[0] * spin_first + fields[1] * spin_second)
    bond_index = jnp.arange(bond, dtype=jnp.int32)
    corner = (bond_index[:, None] == bond - 1) & (bond_index[None, :] == 0)
    base = base + jnp.where(corner[:, :, None, None], onsite[None, None, :, :], jnp.float32(0.0))
    return jnp.pad(base, ((0, padded - bond), (0, padded - bond), (0, 0), (0, 0)))


def on_device(held, owner_map, kept, left_env, mpo_tensor, mpo_mask, fields):
    env_count = lax.axis_size("env")
    core_count = lax.axis_size("col")
    plane_count = lax.axis_size("mpo")
    env_row = lax.axis_index("env")
    core = lax.axis_index("col")
    plane = lax.axis_index("mpo")
    pool, tile, width = held.shape
    sectors_here = kept.shape[0]
    tiles_sector = owner_map.shape[1]
    states = tiles_sector * tile // width
    per_row = sectors_here * tiles_sector
    capacity = 2 * per_row // (env_count * core_count)
    owner_self = env_row * core_count + core
    leading_sector = lax.Precision.HIGHEST
    holder = owner_map // pool
    local_slot = owner_map % pool
    mine = (holder == owner_self).astype(jnp.int32)
    rank = jnp.cumsum(mine, axis=1) - 1
    slot_ids = jnp.arange(capacity, dtype=jnp.int32)
    picked = (mine[:, None, :] == 1) & (rank[:, None, :] == slot_ids[None, :, None])
    source_slot = jnp.sum(jnp.where(picked, local_slot[:, None, :], 0), axis=2)
    part_width = width // plane_count
    source = lax.dynamic_slice_in_dim(held, plane * part_width, part_width, 2)
    outgoing = jnp.take(source, source_slot.reshape(-1), axis=0).reshape(
        env_count, capacity, tile, part_width
    )
    arrived = lax.all_to_all(outgoing, "env", split_axis=0, concat_axis=0, tiled=True)
    arrived = collect(arrived, "col", 1)
    arrived = collect(arrived, "mpo", 3)
    mine_rows = lax.dynamic_slice_in_dim(
        owner_map, env_row * sectors_here, sectors_here, 0
    ).reshape(per_row)
    sender = mine_rows // pool
    position = jnp.arange(per_row, dtype=jnp.int32)
    earlier = (sender[:, None] == sender[None, :]) & (position[None, :] < position[:, None])
    order_within = jnp.sum(earlier.astype(jnp.int32), axis=1)
    index = (
        sender // core_count * (core_count * capacity)
        + sender % core_count * capacity
        + order_within
    )
    flat = arrived.reshape(env_count * core_count * capacity, tile * width)
    sector_matrices = jnp.take(flat, index, axis=0).reshape(sectors_here, states, width, width)
    columns = jnp.arange(width, dtype=jnp.int32)
    keep = columns[None, :] < kept[:, None]
    sector_matrices = jnp.where(
        keep[:, None, None, :], sector_matrices, jnp.zeros((), jnp.bfloat16)
    )
    slab = left_env.shape[0]
    couplings = build_couplings(mpo_tensor, mpo_mask, fields, slab * plane_count)
    share = width // core_count
    own_columns = lax.dynamic_slice_in_dim(sector_matrices, core * share, share, 3)
    mine_coupling = lax.dynamic_slice_in_dim(couplings, plane * slab, slab, 0)
    firsts = jnp.einsum(
        "wij,sja->wsia", left_env[:, 0], own_columns[0], preferred_element_type=jnp.float32
    )
    next_spin = jnp.einsum(
        "wvts,wsia->vtia", mine_coupling, firsts, precision=leading_sector
    ).astype(jnp.bfloat16)
    operator_pieces = [
        jnp.einsum(
            "hze,shzo->seo", sector_matrices[0], next_spin, preferred_element_type=jnp.float32
        )
    ]
    return summed_on_arrival(jnp.stack(operator_pieces, axis=1).astype(jnp.bfloat16), "mpo", 0)


def solution(mesh):
    return jax.shard_map(
        on_device,
        mesh=mesh,
        in_specs=(
            P(("real", "env", "col"), None, None),
            P("real", None),
            P(("real", "env")),
            P("mpo", ("real", "env"), None, None),
            P(),
            P(),
            P("real"),
        ),
        out_specs=P("mpo", ("real", "env"), None, "col"),
        check_vma=False,
    )
```

profile of v0, /device:TPU:33, one launch (start us, length us, event | category | flops | bytes accessed | tf_op | source)
XLA Modules:
  0.0 236.7 jit_solution(11464659930123475766)
XLA Ops:
  0.0 0.9 add_select_fusion
  0.9 0.8 broadcast_compare_fusion
  1.7 0.6 reduce-window.6
  2.9 0.7 fusion.53
  4.2 1.4 fusion.52
  6.0 1.3 constant_dynamic-slice_fusion.1
  7.3 0.7 gather_fusion
  8.3 97.4 %all_to_all.20 = bf16[32,6,8,96]{3,2,1,0:T(8,128)(2,1)S(1)} all-to-all(bf16[32,6,8,96]{3,2,1,0:T(8,128)(2,1)S(1)} %broadcast_select_fusion), channel_id=1, replica_groups=mesh['real'=2,'env'=32,'mpo'=4,'col'=2] {'env'}, dimensions={0} | all-to-all | bytes 589824 | tf_op jit(solution)/shard_map/all_to_all | solution.py:74
  105.8 6.8 %all_to_all.21 = bf16[2,32,6,8,96]{4,3,2,1,0:T(8,128)(2,1)S(1)} all-to-all(bf16[2,32,6,8,96]{4,3,2,1,0:T(8,128)(2,1)S(1)} %broadcast_in_dim.129), channel_id=1, replica_groups=mesh['real'=2,'env'=32,'mpo'=4,'col'=2] {'col'}, dimensions={0} | all-to-all | bytes 1179648 | tf_op jit(solution)/shard_map/all_to_all | solution.py:15
  112.7 2.2 broadcast_in_dim.130
  114.8 5.0 %all-to-all-start.2 = ((bf16[4,32,12,8,96]{4,3,2,1,0:T(8,128)(2,1)}), bf16[4,32,12,8,96]{4,3,2,1,0:T(8,128)(2,1)}, u32[]{:S(2)}, u32[]{:S(2)}) async-start(bf16[4,32,12,8,96]{4,3,2,1,0:T(8,128)(2,1)} %broadcast_in_dim.130), calls=%async_computation.2 | async-start | bytes 6291456 | tf_op jit(solution)/shard_map/all_to_all | solution.py:15
  121.7 1.2 fusion.43
  123.2 0.6 fusion.59
  123.8 33.6 %all-to-all-done.2 = bf16[4,32,12,8,96]{4,3,2,1,0:T(8,128)(2,1)} async-done(((bf16[4,32,12,8,96]{4,3,2,1,0:T(8,128)(2,1)}), bf16[4,32,12,8,96]{4,3,2,1,0:T(8,128)(2,1)}, u32[]{:S(2)}, u32[]{:S(2)}) %all-to-all-start.2) | async-done | bytes 2359328 | tf_op jit(solution)/shard_map/all_to_all | solution.py:15
  157.5 7.6 %copy.34 = bf16[32,12,8,4,96]{4,3,2,1,0:T(4,128)(2,1)} copy(bf16[32,12,8,4,96]{4,2,1,0,3:T(8,128)(2,1)} %bitcast.11) | data formatting | bytes 4718592 | tf_op jit(solution)/shard_map/transpose | solution.py:8
  165.1 7.0 %reshape_reshape.3 = bf16[384,3072]{1,0:T(8,128)(2,1)S(1)} reshape(bf16[32,12,8,4,96]{4,3,2,1,0:T(4,128)(2,1)} %copy.34) | data formatting | bytes 4718592 | tf_op jit(solution)/shard_map/reshape;reshape | solution.py:89
  172.1 2.3 gather_fusion.1
  174.5 2.4 gather.17
  176.8 1.4 gather.18
  178.9 1.4 convolution_bitcast_fusion
  180.4 18.9 %bitcast_convert_fusion = bf16[16,4,384,192]{2,0,3,1:T(8,128)(2,1)S(1)} fusion(f32[4,4,384,192]{2,3,0,1:T(8,128)S(1)} %convolution_bitcast_fusion, f32[4,16,4,4,1]{1,3,0,4,2:T(4,128)S(1)} %copy-done.4), kind=kOutput, calls=%fused_computation.2 | convolution fusion | flops 910688256 | bytes 14159872 | tf_op jit(solution)/shard_map/wvts,wsia->vtia/dot_general | solution.py:104
  199.2 5.3 %bitcast_convert_fusion.1 = bf16[16,192,384]{2,1,0:T(8,128)(2,1)S(1)} fusion(bf16[16,4,384,192]{2,0,3,1:T(8,128)(2,1)S(1)} %bitcast_convert_fusion, bf16[4,384,384]{2,1,0:T(8,128)(2,1)S(1)} %copy-done.2, pred[4,384]{1,0:T(4,128)(4,1)S(1)} %broadcast_in_dim.123, pred[384]{0:T(512)(128)(4,1)S(1)} %iota_compare_fusion.2), kind=kOutput, calls=%fused_computation.5 | convolution fusion | flops 3626237952 | bytes 12978048 | tf_op jit(solution)/shard_map/hze,shzo->seo/dot_general | solution.py:108
  204.5 30.8 %all_to_all.22 = bf16[4,4,1,384,192]{3,4,1,2,0:T(8,128)(2,1)S(1)} all-to-all(bf16[4,4,1,384,192]{3,4,1,2,0:T(8,128)(2,1)S(1)} %bitcast.78), channel_id=1, replica_groups=mesh['real'=2,'env'=32,'mpo'=4,'col'=2] {'mpo'}, dimensions={0} | all-to-all | bytes 4718592 | tf_op jit(solution)/shard_map/all_to_all | solution.py:29
  235.3 1.4 convert_reduce_fusion
  (51 shorter events, 4.1 us)
Async XLA Ops:
  0.0 178.9 %copy-start = (bf16[4,1,384,384]{3,2,1,0:T(8,128)(2,1)S(1)}, bf16[4,1,384,384]{3,2,1,0:T(8,128)(2,1)}, u32[]{:S(2)}) copy-start(bf16[4,1,384,384]{3,2,1,0:T(8,128)(2,1)} %param.10) | copy-start | bytes 3538948
  114.8 6.0 %copy-start.5 = (s32[14,14]{1,0:T(8,128)S(1)}, s32[14,14]{1,0:T(8,128)}, u32[]{:S(2)}) copy-start(s32[14,14]{1,0:T(8,128)} %param.12) | copy-start | bytes 2356
  114.8 6.3 %copy-start.6 = (f32[2]{0:T(128)S(1)}, f32[2]{0:T(128)}, u32[]{:S(2)}) copy-start(f32[2]{0:T(128)} %param.13) | copy-start | bytes 28
  114.8 8.3 %copy-start.3 = (f32[14,14,4,4]{1,3,2,0:T(4,128)S(1)}, f32[14,14,4,4]{1,3,2,0:T(4,128)}, u32[]{:S(2)}) copy-start(f32[14,14,4,4]{1,3,2,0:T(4,128)} %param.11) | copy-start | bytes 37636
  114.8 42.6 %all-to-all-start.2 = ((bf16[4,32,12,8,96]{4,3,2,1,0:T(8,128)(2,1)}), bf16[4,32,12,8,96]{4,3,2,1,0:T(8,128)(2,1)}, u32[]{:S(2)}, u32[]{:S(2)}) async-start(bf16[4,32,12,8,96]{4,3,2,1,0:T(8,128)(2,1)} %broadcast_in_dim.130), calls=%async_computation.2 | async-start | bytes 6291456 | tf_op jit(solution)/shard_map/all_to_all | solution.py:15
  174.5 2.4 %copy-start.1 = (bf16[192,3072]{1,0:T(8,128)(2,1)S(1)}, bf16[192,3072]{1,0:T(8,128)(2,1)}, u32[]{:S(2)}) copy-start(bf16[192,3072]{1,0:T(8,128)(2,1)} %gather_fusion.1) | copy-start | bytes 3538948
  178.9 1.4 copy-start.4
  180.3 18.9 %copy-start.2 = (bf16[4,384,384]{2,1,0:T(8,128)(2,1)S(1)}, bf16[4,384,384]{2,1,0:T(8,128)(2,1)}, u32[]{:S(2)}) copy-start(bf16[4,384,384]{2,1,0:T(8,128)(2,1)} %gather.18) | copy-start | bytes 3538948
where the time goes:
time: 238 us; the launch traced here: 237 us
  blocking collectives  135 us (57%)
  waiting for transfers between devices  33.6 us (14%)
  local copies, waits for them, and re-layouts  28.6 us (12%)
  matrix products  25.6 us (11%)
  other arithmetic  8.04 us (3%)
  starting transfers between devices  5.03 us (2%)
    all_to_all x1, blocking collectives, on_device(): lax.all_to_all(outgoing, 'env', split_axis=0, concat_axis=0, tiled=True)  97.4 us
    all_to_all x1, waiting for transfers between devices, sent_to_all(): return lax.all_to_all(copies, axis, split_axis=0, concat_axis=0, tiled=True)  33.6 us
    all_to_all x1, blocking collectives, summed_on_arrival(): tiles = lax.all_to_all(split_up(shard, dim, count), axis, 0, 0, tiled=True)  30.8 us
    dot_general x1, matrix products, on_device(): jnp.einsum('wvts,wsia->vtia', mine_coupling, firsts, precision=leading_se...  18.9 us
    transpose x1, local copies, waits for them, and re-layouts, in_order(): tiles = jnp.moveaxis(tiles, 0, dim)  7.64 us
    another operation x1, local copies, waits for them, and re-layouts, on_device(): flat = arrived.reshape(env_count * core_count * capacity, tile * width)  7.01 us
    all_to_all x1, blocking collectives, sent_to_all(): return lax.all_to_all(copies, axis, split_axis=0, concat_axis=0, tiled=True)  6.77 us
    gather x3, local copies, waits for them, and re-layouts, on_device(): jnp.take(flat, index, axis=0).reshape(sectors_here, states, width, width)  6.07 us
  transfers between devices with their start and end apart: 1, of which 1 were waited for; matrix products, arithmetic and copies ran while one was open for 1% of the time, Pallas kernels for 0%

commit v1 on v0

v1 whole, which is shorter than its diff:
```python
import functools

import jax
import jax.numpy as jnp
from jax import lax
from jax.experimental import pallas as pl
from jax.experimental.pallas import tpu as pltpu
from jax.sharding import PartitionSpec as P

MESH = pl.DeviceIdType.MESH
VMEM = pltpu.VMEM
SMEM = pltpu.SMEM
DMA = pltpu.SemaphoreType.DMA
LANES = 128
ROWS = 16


def plan_kernel(pool, cap, thirds, sectors, map_ref, src_ref, idx_ref):
    tiles = map_ref.shape[1]
    row = lax.axis_index("env")
    me = row * lax.axis_size("col") + lax.axis_index("col")
    slots = map_ref[...]
    local = slots - me * pool
    mine = (local >= 0) & (local < pool)
    before = lax.broadcasted_iota(jnp.int32, (tiles, tiles), 0) < lax.broadcasted_iota(jnp.int32, (tiles, tiles), 1)
    rank = jnp.dot(
        jnp.where(mine, 1.0, 0.0).astype(jnp.bfloat16),
        jnp.where(before, 1.0, 0.0).astype(jnp.bfloat16),
        preferred_element_type=jnp.float32,
    )
    lane = lax.broadcasted_iota(jnp.int32, src_ref.shape, 1)
    found = jnp.zeros(src_ref.shape, jnp.float32)
    localf = local.astype(jnp.float32)
    for r in range(cap):
        slot = jnp.sum(jnp.where(mine & (rank == float(r)), localf, 0.0), axis=1, keepdims=True)
        found = jnp.where(lane == r, slot, found)
    src_ref[...] = found.astype(jnp.int32)
    own = map_ref[pl.ds(row, 1), :].astype(jnp.float32)
    owner = jnp.floor((own + 0.5) * (1.0 / pool))
    same = lax.broadcasted_iota(jnp.int32, (tiles, tiles), 0) == lax.broadcasted_iota(jnp.int32, (tiles, tiles), 1)
    column = jnp.sum(jnp.where(same, jnp.broadcast_to(owner, (tiles, tiles)), 0.0), axis=1, keepdims=True)
    order = jnp.sum(jnp.where((column == owner) & before, 1.0, 0.0), axis=0, keepdims=True)
    idx_ref[...] = (owner * float(cap * thirds) + order * float(thirds)).astype(jnp.int32)


def main_kernel(
    dims, src_ref, idx_ref, kept_ref, held_ref, left_ref, pair_ref, out_ref,
    units, sent5, sent4, relay5, relay4, lefts, kron, mixed, block, flipped, second,
    load_sem, near5_s, near5_r, near4_s, near4_r, bund_s, bund_r, x_s, x_r, f_s, f_r, d_s, d_r, ls, lr,
):
    n, nx, cap, thirds, bond = dims
    per = cap * thirds
    slab = left_ref.shape[0]
    width = left_ref.shape[2]
    half = n // 2
    hop = n // 4
    z, x, c = lax.axis_index("env"), lax.axis_index("mpo"), lax.axis_index("col")
    states = block.shape[0] // width
    even = lax.rem(x + c, 2) == 0
    sgn = jnp.where(even, 1, -1)

    def start5(p):
        return 4 * p + p // 2

    def start4(p):
        return 5 * p - p // 2

    def at_z(off):
        return lax.rem(z + off + n, n)

    def at_x(off):
        return lax.rem(x + off + nx, nx)

    def rcopy(src, dst, ss, rs, where):
        return pltpu.make_async_remote_copy(src_ref=src, dst_ref=dst, send_sem=ss, recv_sem=rs, device_id=where, device_id_type=MESH)

    load = pltpu.make_async_copy(left_ref, lefts.at[pl.ds(x * slab, slab)], load_sem)
    load.start()

    barrier = pltpu.get_barrier_semaphore()

    def greet(k, _):
        pl.semaphore_signal(barrier, inc=1, device_id={"env": at_z(k)}, device_id_type=MESH)
        pl.semaphore_signal(barrier, inc=1, device_id={"env": at_z(-k)}, device_id_type=MESH)
        return 0

    lax.fori_loop(1, hop + 1, greet, 0)
    pl.semaphore_signal(barrier, inc=1, device_id={"mpo": at_x(1)}, device_id_type=MESH)
    pl.semaphore_signal(barrier, inc=1, device_id={"mpo": at_x(-1)}, device_id_type=MESH)
    pl.semaphore_signal(barrier, inc=1, device_id={"col": 1 - c}, device_id_type=MESH)

    def unit(t, u):
        r, h = u // thirds, lax.rem(u, thirds)
        return held_ref[src_ref[t, r], :, pl.ds(pl.multiple_of(h * LANES, LANES), LANES)]

    u5, u4 = start5(x), start4(x)

    def pick(k, _):
        t5, t4 = at_z(sgn * (k + 1)), at_z(-sgn * (k + 1))
        for i in range(5):
            sent5[k, i] = unit(t5, u5 + i)
        for i in range(4):
            sent4[k, i] = unit(t4, u4 + i)
        return 0

    lax.fori_loop(0, half, pick, 0)

    def own(u, _):
        units[(z * 2 + c) * per + u] = unit(z, u)
        return 0

    lax.fori_loop(0, per, own, 0)

    load.wait()
    pl.semaphore_wait(barrier, 2 * hop + 3)

    def slot(zz, first, count):
        return units.at[pl.ds((zz * 2 + c) * per + first, count)]

    lo = c * (width // 2)

    def rows_of(p, core_lo):
        return lefts.at[pl.ds(p * slab, slab), pl.ds(pl.multiple_of(core_lo, ROWS), width // 2)]

    lsend = []
    for k, off in enumerate((1, -1)):
        cp = rcopy(rows_of(x, lo), rows_of(x, lo), ls.at[k], lr.at[k], {"mpo": at_x(off)})
        cp.start()
        lsend.append(cp)

    far5 = rcopy(sent5.at[pl.ds(hop, hop)], relay5, bund_s.at[0], bund_r.at[0], {"env": at_z(sgn * hop)})
    far4 = rcopy(sent4.at[pl.ds(hop, hop)], relay4, bund_s.at[1], bund_r.at[1], {"env": at_z(-sgn * hop)})
    far5.start()
    far4.start()

    def near_copies(k):
        a = rcopy(sent5.at[k], slot(z, u5, 5), near5_s.at[k], near5_r.at[k], {"env": at_z(sgn * (k + 1))})
        b = rcopy(sent4.at[k], slot(z, u4, 4), near4_s.at[k], near4_r.at[k], {"env": at_z(-sgn * (k + 1))})
        return a, b

    def near(i, _):
        a, b = near_copies(hop - 1 - i)
        a.start()
        b.start()
        return 0

    lax.fori_loop(0, hop, near, 0)

    def d2d(zz, k):
        return rcopy(slot(zz, 0, per), slot(zz, 0, per), d_s.at[k], d_r.at[k], {"col": 1 - c})

    d2d(z, n - 1).start()

    rowi = lax.broadcasted_iota(jnp.int32, (kron.shape[0] // 8, pair_ref.shape[0]), 0)
    coli = lax.broadcasted_iota(jnp.int32, (kron.shape[0] // 8, pair_ref.shape[0]), 1)
    kk = kron.shape[1]
    wi = lax.broadcasted_iota(jnp.int32, (pair_ref.shape[1], kk), 0)
    wc = lax.broadcasted_iota(jnp.int32, (pair_ref.shape[1], kk), 1)
    wk = wc // ROWS + jnp.where(wc < bond * ROWS, 0, pair_ref.shape[1] // 2 - bond)
    spread = jnp.where(wk == wi, 1.0, 0.0).astype(jnp.bfloat16)
    rr = lax.broadcasted_iota(jnp.int32, (kron.shape[0] // 8, kk), 0)
    cc = lax.broadcasted_iota(jnp.int32, (kron.shape[0] // 8, kk), 1)
    diag = lax.rem(rr, ROWS) == lax.rem(cc, ROWS)
    pairs = jnp.dot(pair_ref[...], spread, preferred_element_type=jnp.float32).astype(jnp.bfloat16)

    def build(g, _):
        pickrow = (rowi // ROWS) + g * (kron.shape[0] // 8 // ROWS) == coli
        full = jnp.dot(jnp.where(pickrow, 1.0, 0.0).astype(jnp.bfloat16), pairs, preferred_element_type=jnp.float32)
        kron[pl.ds(g * (kron.shape[0] // 8), kron.shape[0] // 8), :] = jnp.where(diag, full, 0.0).astype(jnp.bfloat16)
        return 0

    lax.fori_loop(0, 8, build, 0)

    fdir = 1 - 2 * c
    pside = {"col": 1 - c}
    from_below = rcopy(rows_of(at_x(-1), lo), rows_of(at_x(-1), lo), ls.at[3], lr.at[3], pside)
    from_above = rcopy(rows_of(at_x(1), lo), rows_of(at_x(1), lo), ls.at[4], lr.at[4], pside)
    lsend[0].wait_recv()
    lsend[1].wait_recv()
    fwd = rcopy(rows_of(at_x(-fdir), lo), rows_of(at_x(-fdir), lo), ls.at[2], lr.at[2], {"mpo": at_x(fdir)})
    fwd.start()
    from_below.start()
    from_above.start()

    def relay_copies(k):
        src5 = at_z(-sgn * hop)
        return rcopy(relay5.at[k], slot(src5, u5, 5), near5_s.at[hop + k], near5_r.at[hop + k], {"env": at_z(sgn * (k + 1))})

    def relay_copies4(k):
        src4 = at_z(sgn * hop)
        return rcopy(relay4.at[k], slot(src4, u4, 4), near4_s.at[hop + k], near4_r.at[hop + k], {"env": at_z(-sgn * (k + 1))})

    far5.wait_recv()
    far4.wait_recv()

    @pl.when(even)
    def _():
        relay_copies(hop - 1).start()

    @pl.when(jnp.logical_not(even))
    def _():
        relay_copies4(hop - 1).start()

    def relay(i, _):
        relay_copies(hop - 2 - i).start()
        relay_copies4(hop - 2 - i).start()
        return 0

    lax.fori_loop(0, hop - 1, relay, 0)

    def x_send(kind, k):
        zz = at_z(-sgn * (k + 1)) if kind == 0 else at_z(sgn * (k + 1))
        ref = slot(zz, u5, 5) if kind == 0 else slot(zz, u4, 4)
        return (
            rcopy(ref, ref, x_s.at[0, kind, k], x_r.at[0, 1 - kind, k], {"mpo": at_x(1)}),
            rcopy(ref, ref, x_s.at[1, kind, k], x_r.at[1, 1 - kind, k], {"mpo": at_x(-1)}),
        )

    def x_wait(side, kind, k):
        zz = at_z(-sgn * (k + 1)) if kind == 0 else at_z(sgn * (k + 1))
        p = at_x(-1) if side == 0 else at_x(1)
        ref = slot(zz, start4(p), 4) if kind == 0 else slot(zz, start5(p), 5)
        return rcopy(ref, ref, x_s.at[side, kind, k], x_r.at[side, kind, k], {"mpo": at_x(1)})

    def f_send(kind, k):
        zz = at_z(-sgn * (k + 1)) if kind == 0 else at_z(sgn * (k + 1))
        p = at_x(-fdir)
        ref = slot(zz, start4(p), 4) if kind == 0 else slot(zz, start5(p), 5)
        return rcopy(ref, ref, f_s.at[kind, k], f_r.at[1 - kind, k], {"mpo": at_x(fdir)})

    def f_wait(kind, k):
        zz = at_z(-sgn * (k + 1)) if kind == 0 else at_z(sgn * (k + 1))
        p = at_x(2)
        ref = slot(zz, start5(p), 5) if kind == 0 else slot(zz, start4(p), 4)
        return rcopy(ref, ref, f_s.at[kind, k], f_r.at[kind, k], {"mpo": at_x(1)})

    def z_wait(kind, k):
        zz = at_z(-sgn * (k + 1)) if kind == 0 else at_z(sgn * (k + 1))
        if kind == 0:
            return rcopy(sent5.at[0], slot(zz, u5, 5), near5_s.at[k], near5_r.at[k], {"env": at_z(1)})
        return rcopy(sent4.at[0], slot(zz, u4, 4), near4_s.at[k], near4_r.at[k], {"env": at_z(1)})

    zhalf = at_z(half)

    def antipode(stage):
        @pl.when(even)
        def _():
            stage(0)

        @pl.when(jnp.logical_not(even))
        def _():
            stage(1)

    kinds = (0, 1)
    last = half - 1

    def one_a(k, kind):
        z_wait(kind, k).wait_recv()
        for cp in x_send(kind, k):
            cp.start()

    def one_b(k, kind):
        x_wait(0, kind, k).wait_recv()
        x_wait(1, kind, k).wait_recv()
        f_send(kind, k).start()

    def stage_a(k, _):
        for kind in kinds:
            one_a(k, kind)
        return 0

    def stage_b(k, _):
        for kind in kinds:
            one_b(k, kind)
        return 0

    def to_other(kind, k):
        zz = at_z(-sgn * (k + 1)) if kind == 0 else at_z(sgn * (k + 1))
        return d2d(zz, 2 * k + kind)

    def stage_c(k, _):
        for kind in kinds:
            f_wait(kind, k).wait_recv()
            to_other(kind, k).start()
        return 0

    lax.fori_loop(0, hop, stage_a, 0)
    lax.fori_loop(0, hop, stage_b, 0)

    fwd_in = rcopy(rows_of(at_x(2), lo), rows_of(at_x(2), lo), ls.at[2], lr.at[2], {"mpo": at_x(1)})
    fwd_in.wait_recv()
    opposite = rcopy(rows_of(at_x(2), lo), rows_of(at_x(2), lo), ls.at[5], lr.at[5], pside)
    opposite.start()

    lax.fori_loop(0, hop, stage_c, 0)

    olo = (1 - c) * (width // 2)
    for k, off in ((3, -1), (4, 1), (5, 2)):
        rcopy(rows_of(at_x(off), olo), rows_of(at_x(off), olo), ls.at[k], lr.at[k], pside).wait_recv()

    step = 2 * ROWS
    chunk = kron.shape[0] // 2

    def mix(i, _):
        r0 = pl.multiple_of(i * step, step)
        a = lefts[0:bond, pl.ds(r0, ROWS), :].reshape(bond * ROWS, width)
        b = lefts[0:bond, pl.ds(r0 + ROWS, ROWS), :].reshape(bond * ROWS, width)
        ab = jnp.concatenate([a, b], axis=1)
        ab = jnp.concatenate([ab, ab], axis=0)
        for g in range(2):
            res = jnp.dot(kron[g * chunk : (g + 1) * chunk, :], ab, preferred_element_type=jnp.float32).astype(jnp.bfloat16)
            for m in range(chunk // ROWS):
                row = g * (chunk // ROWS) + m
                vq, s = row // states, row % states
                part = res[m * ROWS : (m + 1) * ROWS, :]
                mixed[vq, pl.ds(r0, ROWS), s * width : (s + 1) * width] = part[:, :width]
                mixed[vq, pl.ds(r0 + ROWS, ROWS), s * width : (s + 1) * width] = part[:, width:]
        return 0

    nmix = width // step
    lax.fori_loop(0, nmix // 2, mix, 0)
    lax.fori_loop(hop, hop + hop // 2, stage_a, 0)
    lax.fori_loop(nmix // 2, nmix, mix, 0)
    lax.fori_loop(hop + hop // 2, last, stage_a, 0)

    antipode(functools.partial(one_a, last))
    lax.fori_loop(hop, last, stage_b, 0)
    antipode(functools.partial(one_b, last))
    lax.fori_loop(hop, last, stage_c, 0)
    antipode(lambda kind: f_wait(kind, last).wait_recv())
    d2d(zhalf, 2 * last).start()

    def other(zz, k):
        ref = units.at[pl.ds((zz * 2 + 1 - c) * per, per)]
        return rcopy(ref, ref, d_s.at[k], d_r.at[k], pside)

    other(z, n - 1).wait_recv()

    def stage_d(k, _):
        other(at_z(sgn * (k + 1)), 2 * k).wait_recv()
        other(at_z(-sgn * (k + 1)), 2 * k + 1).wait_recv()
        return 0

    lax.fori_loop(0, last, stage_d, 0)
    other(zhalf, 2 * last).wait_recv()

    lane = lax.broadcasted_iota(jnp.int32, (ROWS, LANES), 1)
    masks = [jnp.where(lane + h * LANES < kept_ref[0], 1.0, 0.0).astype(jnp.bfloat16) for h in range(thirds)]

    def place(j, _):
        i0, i1 = idx_ref[0, 2 * j], idx_ref[0, 2 * j + 1]
        for h in range(thirds):
            two = jnp.concatenate([units[i0 + h], units[i1 + h]], axis=0)
            block[pl.ds(pl.multiple_of(j * ROWS, ROWS), ROWS), h * LANES : (h + 1) * LANES] = two * masks[h]
        return 0

    lax.fori_loop(0, block.shape[0] // ROWS, place, 0, unroll=4)

    for k in range(block.shape[0] // LANES):
        flipped[:, k * LANES : (k + 1) * LANES] = block[k * LANES : (k + 1) * LANES, :].T

    nv = second.shape[0]
    cols = second.shape[2]

    def mul(vq, _):
        mine = block[:, pl.ds(pl.multiple_of(c * LANES, LANES), cols)]
        res = jnp.dot(mixed[vq], mine, preferred_element_type=jnp.float32).astype(jnp.bfloat16)
        second[vq // states, pl.ds(pl.multiple_of(lax.rem(vq, states) * width, width), width), :] = res
        return 0

    lax.fori_loop(0, nv * states, mul, 0)
    share = out_ref.shape[2]

    def last_mul(v, _):
        res = jnp.dot(flipped[...], second[v], preferred_element_type=jnp.float32)

        @pl.when(c == 0)
        def _():
            out_ref[v] = res[:, :share]

        @pl.when(c == 1)
        def _():
            out_ref[v] = res[:, cols - share :]

        return 0

    lax.fori_loop(0, nv, last_mul, 0)

    for cp in lsend + [fwd, from_below, from_above, opposite, far5, far4]:
        cp.wait_send()

    def drain(k, _):
        for cp in (
            rcopy(sent5.at[0], sent5.at[0], near5_s.at[k], near5_r.at[k], pside),
            rcopy(sent4.at[0], sent4.at[0], near4_s.at[k], near4_r.at[k], pside),
            *x_send(0, k), *x_send(1, k), f_send(0, k), f_send(1, k), to_other(0, k), to_other(1, k),
        ):
            cp.wait_send()
        return 0

    lax.fori_loop(0, last, drain, 0)

    def drain_last(kind):
        if kind == 0:
            rcopy(sent5.at[0], sent5.at[0], near5_s.at[last], near5_r.at[last], pside).wait_send()
        else:
            rcopy(sent4.at[0], sent4.at[0], near4_s.at[last], near4_r.at[last], pside).wait_send()
        for cp in (*x_send(kind, last), f_send(kind, last)):
            cp.wait_send()

    antipode(drain_last)
    d2d(zhalf, 2 * last).wait_send()
    d2d(z, n - 1).wait_send()


def coupling_rows(mpo_tensor, mpo_mask, fields, first, count):
    bond, states = mpo_tensor.shape[0], mpo_tensor.shape[2]
    base = mpo_tensor * mpo_mask.astype(jnp.float32)[:, :, None, None]
    level = jnp.arange(states, dtype=jnp.int32)
    spin_first = 0.5 - (level // 2).astype(jnp.float32)
    spin_second = 0.5 - (level % 2).astype(jnp.float32)
    onsite = jnp.diag(fields[0] * spin_first + fields[1] * spin_second)
    at = jnp.arange(bond, dtype=jnp.int32)
    corner = (at[:, None] == bond - 1) & (at[None, :] == 0)
    base = base + jnp.where(corner[:, :, None, None], onsite[None, None, :, :], jnp.float32(0.0))
    padded = lax.axis_size("mpo") * count
    base = jnp.pad(base, ((0, padded - bond), (0, padded - bond), (0, 0), (0, 0)))
    rows = lax.dynamic_slice_in_dim(base, first, count, 1)
    rows = jnp.moveaxis(rows, 0, 3).reshape(count * states * states, padded)
    high = lax.reduce_precision(rows, 8, 7)
    return jnp.concatenate([high, rows - high], axis=1).astype(jnp.bfloat16)


def on_device(held, owner_map, kept, left_env, mpo_tensor, mpo_mask, fields):
    n, nx, nc = lax.axis_size("env"), lax.axis_size("mpo"), lax.axis_size("col")
    pool, tile, width = held.shape
    sectors, tiles = owner_map.shape
    states = tiles * tile // width
    cap = 2 * tiles // (n * nc)
    thirds = width // LANES
    slab = left_env.shape[0]
    bond = mpo_tensor.shape[0]
    per = cap * thirds
    half, hop = n // 2, n // 4
    bf16 = jnp.bfloat16

    src, idx = pl.pallas_call(
        functools.partial(plan_kernel, pool, cap, thirds, sectors),
        out_shape=(jax.ShapeDtypeStruct((sectors, 8), jnp.int32), jax.ShapeDtypeStruct((1, tiles), jnp.int32)),
        name="plan",
    )(owner_map)
    pair = coupling_rows(mpo_tensor, mpo_mask, fields, lax.axis_index("mpo") * slab, slab)

    out = pl.pallas_call(
        functools.partial(main_kernel, (n, nx, cap, thirds, bond)),
        out_shape=jax.ShapeDtypeStruct((slab, width, width // nc), jnp.float32),
        in_specs=[
            pl.BlockSpec(memory_space=SMEM),
            pl.BlockSpec(memory_space=SMEM),
            pl.BlockSpec(memory_space=SMEM),
            pl.BlockSpec(memory_space=VMEM),
            pl.BlockSpec(memory_space=pl.ANY),
            pl.BlockSpec(memory_space=VMEM),
        ],
        out_specs=pl.BlockSpec(memory_space=VMEM),
        scratch_shapes=[
            VMEM((n * nc * per, tile, LANES), bf16),
            VMEM((half, 5, tile, LANES), bf16),
            VMEM((half, 4, tile, LANES), bf16),
            VMEM((hop, 5, tile, LANES), bf16),
            VMEM((hop, 4, tile, LANES), bf16),
            VMEM((nx * slab, width, width), bf16),
            VMEM((slab * states * states * ROWS, 2 * bond * ROWS), bf16),
            VMEM((slab * states, width, states * width), bf16),
            VMEM((tiles * tile, width), bf16),
            VMEM((width, tiles * tile), bf16),
            VMEM((slab, states * width, 2 * LANES), bf16),
            DMA,
            DMA((half,)), DMA((half,)), DMA((half,)), DMA((half,)),
            DMA((2,)), DMA((2,)),
            DMA((2, 2, half)), DMA((2, 2, half)),
            DMA((2, half)), DMA((2, half)),
            DMA((n,)), DMA((n,)),
            DMA((6,)), DMA((6,)),
        ],
        compiler_params=pltpu.CompilerParams(collective_id=0, has_side_effects=True, vmem_limit_bytes=56 * 2**20),
        name="exchange_and_contract",
    )(src, idx, kept, held, left_env[:, 0], pair)
    return out[:, None]


def solution(mesh):
    return jax.shard_map(
        on_device,
        mesh=mesh,
        in_specs=(
            P(("real", "env", "col"), None, None),
            P("real", None),
            P(("real", "env")),
            P("mpo", ("real", "env"), None, None),
            P(),
            P(),
            P("real"),
        ),
        out_specs=P("mpo", ("real", "env"), None, "col"),
        check_vma=False,
    )
```

time: 238 us -> 127 us (0.53)
  blocking collectives: 135 us -> 0 us
  Pallas kernels: 0 us -> 118 us
  waiting for transfers between devices: 33.6 us -> 0 us
  matrix products: 25.6 us -> 0 us
  local copies, waits for them, and re-layouts: 28.6 us -> 4.54 us
  starting transfers between devices: 5.03 us -> 0 us
  other arithmetic: 8.04 us -> 3.79 us
    all_to_all x3 -> x0, blocking collectives: 135 us -> none  [the longest x1 97.4 us: on_device(): lax.all_to_all(outgoing, 'env', split_axis=0, concat_axis=0, tiled=True)]
    pallas_call x0 -> x2, Pallas kernels: none -> 118 us  [the longest x1 116 us: on_device(): pl.pallas_call(functools.partial(main_kernel, (n, nx, cap, thirds, bond))...]
    all_to_all x1 -> x0, waiting for transfers between devices: 33.6 us -> none  [sent_to_all(): return lax.all_to_all(copies, axis, split_axis=0, concat_axis=0, tiled=True)]
    dot_general x3 -> x0, matrix products: 25.6 us -> none  [the longest x1 18.9 us: on_device(): jnp.einsum('wvts,wsia->vtia', mine_coupling, firsts, precision=leading_se...]
    transpose x1 -> x2, local copies, waits for them, and re-layouts: 7.64 us -> 0.32 us  [coupling_rows(): rows = jnp.moveaxis(rows, 0, 3).reshape(count * states * states, padded)]
    another operation x2 -> x0, local copies, waits for them, and re-layouts: 7.02 us -> none  [the longest x1 7.01 us: on_device(): flat = arrived.reshape(env_count * core_count * capacity, tile * width)]
    gather x4 -> x0, local copies, waits for them, and re-layouts: 6.81 us -> none  [the longest x3 6.07 us: on_device(): jnp.take(flat, index, axis=0).reshape(sectors_here, states, width, width)]
    all_to_all x1 -> x0, starting transfers between devices: 5.03 us -> none  [sent_to_all(): return lax.all_to_all(copies, axis, split_axis=0, concat_axis=0, tiled=True)]
  transfers between devices with their start and end apart: 1 -> 0, of which waited for: 1 -> 0; matrix products, arithmetic and copies ran while one was open for 1% -> 0% of each run, Pallas kernels for 0% -> 0%
where the time goes in v1:
time: 127 us
  Pallas kernels  118 us (93%)
  local copies, waits for them, and re-layouts  4.54 us (4%)
  other arithmetic  3.79 us (3%)
    pallas_call x1, Pallas kernels, on_device(): pl.pallas_call(functools.partial(main_kernel, (n, nx, cap, thirds, bond))...  116 us
    broadcast_in_dim x1, local copies, waits for them, and re-layouts, on_device(): return out[:, None]  2.88 us

profile of v1, /device:TPU:33, one launch (start us, length us, event | category | flops | bytes accessed | tf_op | source)
XLA Modules:
  0.0 127.1 jit_solution(13370376487348321771)
XLA Ops:
  0.7 1.3 %fusion.9 = (f32[1]{0:T(128)}, f32[1]{0:T(128)}) fusion(f32[2]{0:T(128)} %param.13), kind=kLoop, calls=%fused_computation.23 | loop fusion | bytes 16 | tf_op jit(solution)/shard_map/slice | solution.py:422
  2.0 1.3 fusion.5
  3.3 0.1 broadcast_and_fusion
  3.3 0.1 fusion.1
  3.4 0.7 convert_element_type.20
  4.1 1.6 %plan.1 = (s32[32,8]{1,0:T(8,128)}, s32[1,192]{1,0:T(1,128)}) custom-call(s32[32,192]{1,0:T(8,128)} %map_ref.1), custom_call_target="tpu_custom_call" | custom-call | tf_op jit(solution)/shard_map/plan/pallas_call | solution.py:447
  5.7 1.0 select_add_fusion
  6.7 0.1 dynamic-slice_bitcast_fusion
  6.9 0.2 copy.8
  7.1 0.7 pad_maximum_fusion.pair_ref
  7.7 116.5 %exchange_and_contract.1 = f32[4,384,192]{2,1,0:T(8,128)} custom-call(s32[32,8]{1,0:T(8,128)} %get-tuple-element.7.src_ref, s32[1,192]{1,0:T(1,128)} %get-tuple-element.8.idx_ref, s32[1]{0:T(128)S(6)} %copy.10.kept_ref, bf16[192,8,384]{2,1,0:T(8,128)(2,1)} %held_ref.1, bf16[4,384,384]{2,1,0:T(8,128)(2,1)} %bitcast.8, bf16[64,32]{1,0:T(8,128)(2,1)} %pad_maximum_fusion.pair_ref), custom_call_target="tpu_custom_call" | custom-call | tf_op jit(solution)/shard_map/exchange_and_contract/pallas_call | solution.py:454
  124.2 2.9 %copy.9 = f32[4,1,384,192]{2,3,1,0:T(8,128)} copy(f32[4,1,384,192]{3,2,0,1:T(8,128)} %bitcast.7) | data formatting | bytes 2359296 | tf_op jit(solution)/shard_map/broadcast_in_dim | solution.py:489
  (2 shorter events, 0.0 us)

commit v2 on v1

--- a/solution.py
+++ b/solution.py
@@ -44,9 +44,10 @@
 
 
 def main_kernel(
-    dims, src_ref, idx_ref, kept_ref, held_ref, left_ref, pair_ref, out_ref,
+    dims, src_ref, idx_ref, kept_ref, fields_ref, held_ref, left_ref, mpo_ref, mask_ref, out_ref,
     units, sent5, sent4, relay5, relay4, lefts, kron, mixed, block, flipped, second,
-    load_sem, near5_s, near5_r, near4_s, near4_r, bund_s, bund_r, x_s, x_r, f_s, f_r, d_s, d_r, ls, lr,
+    load_sem, near5_s, near5_r, near4_s, near4_r, bund_s, bund_r, x_s, x_r, f_s, f_r, d_s, d_r,
+    ln_s, ln_r, lf_s, lf_r, lp_s, lp_r,
 ):
     n, nx, cap, thirds, bond = dims
     per = cap * thirds
@@ -117,16 +118,52 @@
     def slot(zz, first, count):
         return units.at[pl.ds((zz * 2 + c) * per + first, count)]
 
-    lo = c * (width // 2)
-
-    def rows_of(p, core_lo):
-        return lefts.at[pl.ds(p * slab, slab), pl.ds(pl.multiple_of(core_lo, ROWS), width // 2)]
-
-    lsend = []
-    for k, off in enumerate((1, -1)):
-        cp = rcopy(rows_of(x, lo), rows_of(x, lo), ls.at[k], lr.at[k], {"mpo": at_x(off)})
-        cp.start()
-        lsend.append(cp)
+    parts = ln_s.shape[1]
+    piece = width // 2 // parts
+    fdir = 1 - 2 * c
+    pside = {"col": 1 - c}
+
+    def rows_of(p, core, g):
+        first = pl.multiple_of(core * (width // 2) + g * piece, ROWS)
+        return lefts.at[pl.ds(p * slab, slab), pl.ds(first, piece)]
+
+    def l_own(g):
+        ref = rows_of(x, c, g)
+        return [rcopy(ref, ref, ln_s.at[k, g], ln_r.at[k, g], {"mpo": at_x(off)}) for k, off in ((0, 1), (1, -1))]
+
+    def l_fwd(g):
+        ref = rows_of(at_x(-fdir), c, g)
+        return rcopy(ref, ref, lf_s.at[g], lf_r.at[g], {"mpo": at_x(fdir)})
+
+    def l_pair(k, g, core):
+        ref = rows_of(at_x((-1, 1, 2)[k]), core, g)
+        return rcopy(ref, ref, lp_s.at[k, g], lp_r.at[k, g], pside)
+
+    def l_start(g):
+        for cp in l_own(g):
+            cp.start()
+
+    def l_serve(g):
+        for k, off in ((0, -1), (1, 1)):
+            ref = rows_of(at_x(off), c, g)
+            rcopy(ref, ref, ln_s.at[k, g], ln_r.at[k, g], pside).wait_recv()
+        l_fwd(g).start()
+        if g + 2 < parts:
+            l_start(g + 2)
+        l_pair(0, g, c).start()
+        l_pair(1, g, c).start()
+
+    def l_finish(g):
+        ref = rows_of(at_x(2), c, g)
+        rcopy(ref, ref, lf_s.at[g], lf_r.at[g], pside).wait_recv()
+        l_pair(2, g, c).start()
+
+    def l_ready(g):
+        for k in range(3):
+            l_pair(k, g, 1 - c).wait_recv()
+
+    l_start(0)
+    l_start(1)
 
     far5 = rcopy(sent5.at[pl.ds(hop, hop)], relay5, bund_s.at[0], bund_r.at[0], {"env": at_z(sgn * hop)})
     far4 = rcopy(sent4.at[pl.ds(hop, hop)], relay4, bund_s.at[1], bund_r.at[1], {"env": at_z(-sgn * hop)})
@@ -151,36 +188,69 @@
 
     d2d(z, n - 1).start()
 
-    rowi = lax.broadcasted_iota(jnp.int32, (kron.shape[0] // 8, pair_ref.shape[0]), 0)
-    coli = lax.broadcasted_iota(jnp.int32, (kron.shape[0] // 8, pair_ref.shape[0]), 1)
+    rows, vees = mpo_ref.shape
+    ss = states * states
+    own_v = slab
+    bf16, f32 = jnp.bfloat16, jnp.float32
+
+    def iota(shape, dim):
+        return lax.broadcasted_iota(jnp.int32, shape, dim)
+
+    def ones(cond):
+        return jnp.where(cond, 1.0, 0.0).astype(bf16)
+
+    wrow = ones(iota((rows, bond), 0) // ss == iota((rows, bond), 1))
+    base = mpo_ref[...] * jnp.dot(wrow, mask_ref[...].astype(f32).astype(bf16), preferred_element_type=f32)
+    ri, li = iota((rows, vees), 0), iota((rows, vees), 1)
+    qi, si = lax.rem(ri, ss) // states, lax.rem(ri, states)
+    onsite = fields_ref[0] * (0.5 - (si // 2).astype(f32)) + fields_ref[1] * (0.5 - lax.rem(si, 2).astype(f32))
+    base = base + jnp.where((ri >= (bond - 1) * ss) & (qi == si) & (li == 0), onsite, 0.0)
+    high = base.astype(bf16)
+    low = (base - high.astype(f32)).astype(bf16)
+    nrow = ss * own_v
+    select = ones(iota((nrow, vees), 1) == x * own_v + lax.rem(iota((nrow, vees), 0), own_v))
+    match = lax.rem(iota((nrow, rows), 1), ss) == iota((nrow, rows), 0) // own_v
+    spread = ones(iota((rows, bond * ROWS), 0) // ss == iota((rows, bond * ROWS), 1) // ROWS)
+
+    def per_row(m):
+        picked = lax.dot_general(select, m, (((1,), (1,)), ((), ())), preferred_element_type=f32)
+        return jnp.dot(jnp.where(match, picked, 0.0).astype(bf16), spread, preferred_element_type=f32).astype(bf16)
+
+    pairs = jnp.concatenate([per_row(high), per_row(low)], axis=1)
     kk = kron.shape[1]
-    wi = lax.broadcasted_iota(jnp.int32, (pair_ref.shape[1], kk), 0)
-    wc = lax.broadcasted_iota(jnp.int32, (pair_ref.shape[1], kk), 1)
-    wk = wc // ROWS + jnp.where(wc < bond * ROWS, 0, pair_ref.shape[1] // 2 - bond)
-    spread = jnp.where(wk == wi, 1.0, 0.0).astype(jnp.bfloat16)
-    rr = lax.broadcasted_iota(jnp.int32, (kron.shape[0] // 8, kk), 0)
-    cc = lax.broadcasted_iota(jnp.int32, (kron.shape[0] // 8, kk), 1)
-    diag = lax.rem(rr, ROWS) == lax.rem(cc, ROWS)
-    pairs = jnp.dot(pair_ref[...], spread, preferred_element_type=jnp.float32).astype(jnp.bfloat16)
+    group = kron.shape[0] // 8
+    diag = lax.rem(iota((group, kk), 0), ROWS) == lax.rem(iota((group, kk), 1), ROWS)
 
     def build(g, _):
-        pickrow = (rowi // ROWS) + g * (kron.shape[0] // 8 // ROWS) == coli
-        full = jnp.dot(jnp.where(pickrow, 1.0, 0.0).astype(jnp.bfloat16), pairs, preferred_element_type=jnp.float32)
-        kron[pl.ds(g * (kron.shape[0] // 8), kron.shape[0] // 8), :] = jnp.where(diag, full, 0.0).astype(jnp.bfloat16)
+        row = ones(iota((group, nrow), 0) // ROWS + g * (group // ROWS) == iota((group, nrow), 1))
+        full = jnp.dot(row, pairs, preferred_element_type=f32)
+        kron[pl.ds(g * group, group), :] = jnp.where(diag, full, 0.0).astype(bf16)
         return 0
 
     lax.fori_loop(0, 8, build, 0)
 
-    fdir = 1 - 2 * c
-    pside = {"col": 1 - c}
-    from_below = rcopy(rows_of(at_x(-1), lo), rows_of(at_x(-1), lo), ls.at[3], lr.at[3], pside)
-    from_above = rcopy(rows_of(at_x(1), lo), rows_of(at_x(1), lo), ls.at[4], lr.at[4], pside)
-    lsend[0].wait_recv()
-    lsend[1].wait_recv()
-    fwd = rcopy(rows_of(at_x(-fdir), lo), rows_of(at_x(-fdir), lo), ls.at[2], lr.at[2], {"mpo": at_x(fdir)})
-    fwd.start()
-    from_below.start()
-    from_above.start()
+    chunk = kron.shape[0] // 2
+
+    def mix(g):
+        def one(t, _):
+            r0 = pl.multiple_of(g * piece + t * ROWS, ROWS)
+            r1 = pl.multiple_of(r0 + width // 2, ROWS)
+            a = lefts[0:bond, pl.ds(r0, ROWS), :].reshape(bond * ROWS, width)
+            b = lefts[0:bond, pl.ds(r1, ROWS), :].reshape(bond * ROWS, width)
+            ab = jnp.concatenate([a, b], axis=1)
+            ab = jnp.concatenate([ab, ab], axis=0)
+            for e in range(2):
+                res = jnp.dot(kron[e * chunk : (e + 1) * chunk, :], ab, preferred_element_type=f32).astype(bf16)
+                for m in range(chunk // ROWS):
+                    row = e * (chunk // ROWS) + m
+                    qs, v = row // own_v, row % own_v
+                    vq, s = v * states + qs // states, qs % states
+                    part = res[m * ROWS : (m + 1) * ROWS, :]
+                    mixed[vq, pl.ds(r0, ROWS), s * width : (s + 1) * width] = part[:, :width]
+                    mixed[vq, pl.ds(r1, ROWS), s * width : (s + 1) * width] = part[:, width:]
+            return 0
+
+        lax.fori_loop(0, piece // ROWS, one, 0)
 
     def relay_copies(k):
         src5 = at_z(-sgn * hop)
@@ -190,23 +260,24 @@
         src4 = at_z(sgn * hop)
         return rcopy(relay4.at[k], slot(src4, u4, 4), near4_s.at[hop + k], near4_r.at[hop + k], {"env": at_z(-sgn * (k + 1))})
 
-    far5.wait_recv()
-    far4.wait_recv()
-
-    @pl.when(even)
-    def _():
-        relay_copies(hop - 1).start()
-
-    @pl.when(jnp.logical_not(even))
-    def _():
-        relay_copies4(hop - 1).start()
-
-    def relay(i, _):
-        relay_copies(hop - 2 - i).start()
-        relay_copies4(hop - 2 - i).start()
-        return 0
-
-    lax.fori_loop(0, hop - 1, relay, 0)
+    def serve_relay():
+        far5.wait_recv()
+        far4.wait_recv()
+
+        @pl.when(even)
+        def _():
+            relay_copies(hop - 1).start()
+
+        @pl.when(jnp.logical_not(even))
+        def _():
+            relay_copies4(hop - 1).start()
+
+        def relay(i, _):
+            relay_copies(hop - 2 - i).start()
+            relay_copies4(hop - 2 - i).start()
+            return 0
+
+        lax.fori_loop(0, hop - 1, relay, 0)
 
     def x_send(kind, k):
         zz = at_z(-sgn * (k + 1)) if kind == 0 else at_z(sgn * (k + 1))
@@ -284,49 +355,41 @@
             to_other(kind, k).start()
         return 0
 
+    l_serve(0)
+    l_serve(1)
+    l_finish(0)
+    l_serve(2)
+    l_finish(1)
+    l_ready(0)
+    mix(0)
+    l_serve(3)
+    l_finish(2)
+    l_ready(1)
+    serve_relay()
+    mix(1)
     lax.fori_loop(0, hop, stage_a, 0)
+    l_finish(3)
+    l_ready(2)
+    mix(2)
     lax.fori_loop(0, hop, stage_b, 0)
-
-    fwd_in = rcopy(rows_of(at_x(2), lo), rows_of(at_x(2), lo), ls.at[2], lr.at[2], {"mpo": at_x(1)})
-    fwd_in.wait_recv()
-    opposite = rcopy(rows_of(at_x(2), lo), rows_of(at_x(2), lo), ls.at[5], lr.at[5], pside)
-    opposite.start()
-
-    lax.fori_loop(0, hop, stage_c, 0)
-
-    olo = (1 - c) * (width // 2)
-    for k, off in ((3, -1), (4, 1), (5, 2)):
-        rcopy(rows_of(at_x(off), olo), rows_of(at_x(off), olo), ls.at[k], lr.at[k], pside).wait_recv()
-
-    step = 2 * ROWS
-    chunk = kron.shape[0] // 2
-
-    def mix(i, _):
-        r0 = pl.multiple_of(i * step, step)
-        a = lefts[0:bond, pl.ds(r0, ROWS), :].reshape(bond * ROWS, width)
-        b = lefts[0:bond, pl.ds(r0 + ROWS, ROWS), :].reshape(bond * ROWS, width)
-        ab = jnp.concatenate([a, b], axis=1)
-        ab = jnp.concatenate([ab, ab], axis=0)
-        for g in range(2):
-            res = jnp.dot(kron[g * chunk : (g + 1) * chunk, :], ab, preferred_element_type=jnp.float32).astype(jnp.bfloat16)
-            for m in range(chunk // ROWS):
-                row = g * (chunk // ROWS) + m
-                vq, s = row // states, row % states
-                part = res[m * ROWS : (m + 1) * ROWS, :]
-                mixed[vq, pl.ds(r0, ROWS), s * width : (s + 1) * width] = part[:, :width]
-                mixed[vq, pl.ds(r0 + ROWS, ROWS), s * width : (s + 1) * width] = part[:, width:]
-        return 0
-
-    nmix = width // step
-    lax.fori_loop(0, nmix // 2, mix, 0)
-    lax.fori_loop(hop, hop + hop // 2, stage_a, 0)
-    lax.fori_loop(nmix // 2, nmix, mix, 0)
-    lax.fori_loop(hop + hop // 2, last, stage_a, 0)
-
-    antipode(functools.partial(one_a, last))
-    lax.fori_loop(hop, last, stage_b, 0)
-    antipode(functools.partial(one_b, last))
-    lax.fori_loop(hop, last, stage_c, 0)
+    l_ready(3)
+    mix(3)
+    lag = 2
+    for k in range(hop, last + 1 + 2 * lag):
+        if k < last:
+            stage_a(k, 0)
+        elif k == last:
+            antipode(functools.partial(one_a, last))
+        if k == hop + 1:
+            lax.fori_loop(0, hop, stage_c, 0)
+        kb = k - lag
+        if hop <= kb < last:
+            stage_b(kb, 0)
+        elif kb == last:
+            antipode(functools.partial(one_b, last))
+        kc = k - 2 * lag
+        if hop <= kc < last:
+            stage_c(kc, 0)
     antipode(lambda kind: f_wait(kind, last).wait_recv())
     d2d(zhalf, 2 * last).start()
 
@@ -356,38 +419,42 @@
 
     lax.fori_loop(0, block.shape[0] // ROWS, place, 0, unroll=4)
 
-    for k in range(block.shape[0] // LANES):
-        flipped[:, k * LANES : (k + 1) * LANES] = block[k * LANES : (k + 1) * LANES, :].T
-
     nv = second.shape[0]
     cols = second.shape[2]
-
-    def mul(vq, _):
+    turns = block.shape[0] // LANES // nv
+
+    def mul(v, _):
         mine = block[:, pl.ds(pl.multiple_of(c * LANES, LANES), cols)]
-        res = jnp.dot(mixed[vq], mine, preferred_element_type=jnp.float32).astype(jnp.bfloat16)
-        second[vq // states, pl.ds(pl.multiple_of(lax.rem(vq, states) * width, width), width), :] = res
-        return 0
-
-    lax.fori_loop(0, nv * states, mul, 0)
-    share = out_ref.shape[2]
+        lhs = mixed[pl.ds(v * states, states)].reshape(states * width, states * width)
+        second[v] = jnp.dot(lhs, mine, preferred_element_type=f32).astype(bf16)
+        for k in range(turns):
+            at = pl.multiple_of((v * turns + k) * LANES, LANES)
+            flipped[:, pl.ds(at, LANES)] = block[pl.ds(at, LANES), :].T
+        return 0
+
+    lax.fori_loop(0, nv, mul, 0)
+    share = out_ref.shape[1]
 
     def last_mul(v, _):
-        res = jnp.dot(flipped[...], second[v], preferred_element_type=jnp.float32)
+        res = jnp.dot(flipped[...], second[v], preferred_element_type=f32).T
 
         @pl.when(c == 0)
         def _():
-            out_ref[v] = res[:, :share]
+            out_ref[v] = res[:share]
 
         @pl.when(c == 1)
         def _():
-            out_ref[v] = res[:, cols - share :]
+            out_ref[v] = res[cols - share :]
 
         return 0
 
     lax.fori_loop(0, nv, last_mul, 0)
 
-    for cp in lsend + [fwd, from_below, from_above, opposite, far5, far4]:
-        cp.wait_send()
+    far5.wait_send()
+    far4.wait_send()
+    for g in range(parts):
+        for cp in (*l_own(g), l_fwd(g), l_pair(0, g, c), l_pair(1, g, c), l_pair(2, g, c)):
+            cp.wait_send()
 
     def drain(k, _):
         for cp in (
@@ -411,24 +478,6 @@
     antipode(drain_last)
     d2d(zhalf, 2 * last).wait_send()
     d2d(z, n - 1).wait_send()
-
-
-def coupling_rows(mpo_tensor, mpo_mask, fields, first, count):
-    bond, states = mpo_tensor.shape[0], mpo_tensor.shape[2]
-    base = mpo_tensor * mpo_mask.astype(jnp.float32)[:, :, None, None]
-    level = jnp.arange(states, dtype=jnp.int32)
-    spin_first = 0.5 - (level // 2).astype(jnp.float32)
-    spin_second = 0.5 - (level % 2).astype(jnp.float32)
-    onsite = jnp.diag(fields[0] * spin_first + fields[1] * spin_second)
-    at = jnp.arange(bond, dtype=jnp.int32)
-    corner = (at[:, None] == bond - 1) & (at[None, :] == 0)
-    base = base + jnp.where(corner[:, :, None, None], onsite[None, None, :, :], jnp.float32(0.0))
-    padded = lax.axis_size("mpo") * count
-    base = jnp.pad(base, ((0, padded - bond), (0, padded - bond), (0, 0), (0, 0)))
-    rows = lax.dynamic_slice_in_dim(base, first, count, 1)
-    rows = jnp.moveaxis(rows, 0, 3).reshape(count * states * states, padded)
-    high = lax.reduce_precision(rows, 8, 7)
-    return jnp.concatenate([high, rows - high], axis=1).astype(jnp.bfloat16)
 
 
 def on_device(held, owner_map, kept, left_env, mpo_tensor, mpo_mask, fields):
@@ -449,17 +498,19 @@
         out_shape=(jax.ShapeDtypeStruct((sectors, 8), jnp.int32), jax.ShapeDtypeStruct((1, tiles), jnp.int32)),
         name="plan",
     )(owner_map)
-    pair = coupling_rows(mpo_tensor, mpo_mask, fields, lax.axis_index("mpo") * slab, slab)
+    mpo_rows = jnp.transpose(mpo_tensor, (0, 2, 3, 1)).reshape(bond * states * states, bond)
 
     out = pl.pallas_call(
         functools.partial(main_kernel, (n, nx, cap, thirds, bond)),
-        out_shape=jax.ShapeDtypeStruct((slab, width, width // nc), jnp.float32),
+        out_shape=jax.ShapeDtypeStruct((slab, width // nc, width), jnp.float32),
         in_specs=[
+            pl.BlockSpec(memory_space=SMEM),
             pl.BlockSpec(memory_space=SMEM),
             pl.BlockSpec(memory_space=SMEM),
             pl.BlockSpec(memory_space=SMEM),
             pl.BlockSpec(memory_space=VMEM),
             pl.BlockSpec(memory_space=pl.ANY),
+            pl.BlockSpec(memory_space=VMEM),
             pl.BlockSpec(memory_space=VMEM),
         ],
         out_specs=pl.BlockSpec(memory_space=VMEM),
@@ -481,12 +532,12 @@
             DMA((2, 2, half)), DMA((2, 2, half)),
             DMA((2, half)), DMA((2, half)),
             DMA((n,)), DMA((n,)),
-            DMA((6,)), DMA((6,)),
+            DMA((2, 4)), DMA((2, 4)), DMA((4,)), DMA((4,)), DMA((3, 4)), DMA((3, 4)),
         ],
         compiler_params=pltpu.CompilerParams(collective_id=0, has_side_effects=True, vmem_limit_bytes=56 * 2**20),
         name="exchange_and_contract",
-    )(src, idx, kept, held, left_env[:, 0], pair)
-    return out[:, None]
+    )(src, idx, kept, fields, held, left_env[:, 0], mpo_rows, mpo_mask)
+    return jnp.swapaxes(out, 1, 2)[:, None]
 
 
 def solution(mesh):

time: 127 us -> 112 us (0.88)
  Pallas kernels: 118 us -> 109 us
  other arithmetic: 3.79 us -> 0 us
  local copies, waits for them, and re-layouts: 4.54 us -> 2.36 us
    pallas_call x1, Pallas kernels: 116 us -> 107 us  [on_device(): pl.pallas_call(functools.partial(main_kernel, (n, nx, cap, thirds, bond))...]
    broadcast_in_dim x1 -> x0, local copies, waits for them, and re-layouts: 2.88 us -> none  [on_device(): return out[:, None]]
    unnamed x0 -> x1, local copies, waits for them, and re-layouts: none -> 2.36 us
    add x2 -> x0, other arithmetic: 2.24 us -> none  [the longest x1 1.26 us: coupling_rows(): onsite = jnp.diag(fields[0] * spin_first + fields[1] * spin_second)]
    slice x1 -> x0, local copies, waits for them, and re-layouts: 1.34 us -> none  [coupling_rows(): onsite = jnp.diag(fields[0] * spin_first + fields[1] * spin_second)]
where the time goes in v2:
time: 112 us
  Pallas kernels  109 us (97%)
  local copies, waits for them, and re-layouts  2.36 us (2%)
    pallas_call x1, Pallas kernels, on_device(): pl.pallas_call(functools.partial(main_kernel, (n, nx, cap, thirds, bond))...  107 us
    unnamed x1, local copies, waits for them, and re-layouts  2.36 us

profile of v2, /device:TPU:33, one launch (start us, length us, event | category | flops | bytes accessed | tf_op | source)
XLA Modules:
  0.0 111.9 jit_solution(18420259897965297881)
XLA Ops:
  0.7 1.6 %plan.1 = (s32[32,8]{1,0:T(8,128)}, s32[1,192]{1,0:T(1,128)}) custom-call(s32[32,192]{1,0:T(8,128)} %map_ref.1), custom_call_target="tpu_custom_call" | custom-call | tf_op jit(solution)/shard_map/plan/pallas_call | solution.py:496
  2.3 107.3 %exchange_and_contract.1 = f32[4,192,384]{2,1,0:T(8,128)} custom-call(s32[32,8]{1,0:T(8,128)} %get-tuple-element.7.src_ref, s32[1,192]{1,0:T(1,128)} %get-tuple-element.8.idx_ref, s32[1]{0:T(128)S(6)} %copy.10.kept_ref, f32[2]{0:T(128)} %fields_ref.1, bf16[192,8,384]{2,1,0:T(8,128)(2,1)} %held_ref.1, bf16[4,384,384]{2,1,0:T(8,128)(2,1)} %bitcast.10, ...), custom_call_target="tpu_custom_call" | custom-call | tf_op jit(solution)/shard_map/exchange_and_contract/pallas_call | solution.py:503
  109.6 2.4 %copy.11 = f32[4,1,384,192]{2,3,1,0:T(8,128)} copy(f32[4,1,384,192]{2,3,1,0:T(8,128)} %bitcast.9) | data formatting | bytes 2359296

commit v3 on v2

--- a/solution.py
+++ b/solution.py
@@ -13,6 +13,7 @@
 DMA = pltpu.SemaphoreType.DMA
 LANES = 128
 ROWS = 16
+BUNDLES = 2
 
 
 def plan_kernel(pool, cap, thirds, sectors, map_ref, src_ref, idx_ref):
@@ -44,9 +45,9 @@
 
 
 def main_kernel(
-    dims, src_ref, idx_ref, kept_ref, fields_ref, held_ref, left_ref, mpo_ref, mask_ref, out_ref,
-    units, sent5, sent4, relay5, relay4, lefts, kron, mixed, block, flipped, second,
-    load_sem, near5_s, near5_r, near4_s, near4_r, bund_s, bund_r, x_s, x_r, f_s, f_r, d_s, d_r,
+    dims, src_ref, idx_ref, kept_ref, fields_ref, pool_ref, left_ref, mpo_ref, mask_ref, out_ref,
+    held_ref, units, sent5, sent4, relay5, relay4, lefts, kron, mixed, block, flipped, second,
+    load_sem, pool_sem, near5_s, near5_r, near4_s, near4_r, bund_s, bund_r, x_s, x_r, f_s, f_r, d_s, d_r,
     ln_s, ln_r, lf_s, lf_r, lp_s, lp_r,
 ):
     n, nx, cap, thirds, bond = dims
@@ -75,6 +76,8 @@
     def rcopy(src, dst, ss, rs, where):
         return pltpu.make_async_remote_copy(src_ref=src, dst_ref=dst, send_sem=ss, recv_sem=rs, device_id=where, device_id_type=MESH)
 
+    fetch = pltpu.make_async_copy(pool_ref, held_ref, pool_sem)
+    fetch.start()
     load = pltpu.make_async_copy(left_ref, lefts.at[pl.ds(x * slab, slab)], load_sem)
     load.start()
 
@@ -98,12 +101,14 @@
 
     def pick(k, _):
         t5, t4 = at_z(sgn * (k + 1)), at_z(-sgn * (k + 1))
+        first = jnp.where(jnp.logical_and(k == half - 1, jnp.logical_not(even)), u4, u5)
         for i in range(5):
-            sent5[k, i] = unit(t5, u5 + i)
+            sent5[k, i] = unit(t5, first + i)
         for i in range(4):
             sent4[k, i] = unit(t4, u4 + i)
         return 0
 
+    fetch.wait()
     lax.fori_loop(0, half, pick, 0)
 
     def own(u, _):
@@ -165,10 +170,18 @@
     l_start(0)
     l_start(1)
 
-    far5 = rcopy(sent5.at[pl.ds(hop, hop)], relay5, bund_s.at[0], bund_r.at[0], {"env": at_z(sgn * hop)})
-    far4 = rcopy(sent4.at[pl.ds(hop, hop)], relay4, bund_s.at[1], bund_r.at[1], {"env": at_z(-sgn * hop)})
-    far5.start()
-    far4.start()
+    step = hop // BUNDLES
+
+    def bundle(b):
+        n4 = step - 1 if b == BUNDLES - 1 else step
+        return (
+            rcopy(sent5.at[pl.ds(hop + b * step, step)], relay5.at[pl.ds(b * step, step)], bund_s.at[0, b], bund_r.at[0, b], {"env": at_z(sgn * hop)}),
+            rcopy(sent4.at[pl.ds(hop + b * step, n4)], relay4.at[pl.ds(b * step, n4)], bund_s.at[1, b], bund_r.at[1, b], {"env": at_z(-sgn * hop)}),
+        )
+
+    for b in range(BUNDLES - 1, -1, -1):
+        for cp in bundle(b):
+            cp.start()
 
     def near_copies(k):
         a = rcopy(sent5.at[k], slot(z, u5, 5), near5_s.at[k], near5_r.at[k], {"env": at_z(sgn * (k + 1))})
@@ -256,28 +269,23 @@
         src5 = at_z(-sgn * hop)
         return rcopy(relay5.at[k], slot(src5, u5, 5), near5_s.at[hop + k], near5_r.at[hop + k], {"env": at_z(sgn * (k + 1))})
 
+    def relay_last4():
+        return rcopy(relay5.at[hop - 1, pl.ds(0, 4)], slot(at_z(-sgn * hop), u4, 4), near4_s.at[half - 1], near4_r.at[half - 1], {"env": at_z(sgn * hop)})
+
     def relay_copies4(k):
         src4 = at_z(sgn * hop)
         return rcopy(relay4.at[k], slot(src4, u4, 4), near4_s.at[hop + k], near4_r.at[hop + k], {"env": at_z(-sgn * (k + 1))})
 
-    def serve_relay():
-        far5.wait_recv()
-        far4.wait_recv()
-
-        @pl.when(even)
-        def _():
-            relay_copies(hop - 1).start()
-
-        @pl.when(jnp.logical_not(even))
-        def _():
-            relay_copies4(hop - 1).start()
-
-        def relay(i, _):
-            relay_copies(hop - 2 - i).start()
-            relay_copies4(hop - 2 - i).start()
-            return 0
-
-        lax.fori_loop(0, hop - 1, relay, 0)
+    def serve_relay(b):
+        for cp in bundle(b):
+            cp.wait_recv()
+        for k in range((b + 1) * step - 1, b * step - 1, -1):
+            if k < hop - 1:
+                relay_copies(k).start()
+                relay_copies4(k).start()
+            else:
+                pl.when(even)(relay_copies(k).start)
+                pl.when(jnp.logical_not(even))(relay_last4().start)
 
     def x_send(kind, k):
         zz = at_z(-sgn * (k + 1)) if kind == 0 else at_z(sgn * (k + 1))
@@ -355,6 +363,12 @@
             to_other(kind, k).start()
         return 0
 
+    def backwards(stage, top):
+        lax.fori_loop(0, hop, lambda i, _: stage(top - 1 - i, 0), 0)
+
+    def far(stage):
+        lax.fori_loop(0, last - hop, lambda i, _: stage(last - 1 - i, 0), 0)
+
     l_serve(0)
     l_serve(1)
     l_finish(0)
@@ -362,36 +376,27 @@
     l_finish(1)
     l_ready(0)
     mix(0)
+    for b in range(BUNDLES - 1, -1, -1):
+        serve_relay(b)
     l_serve(3)
     l_finish(2)
     l_ready(1)
-    serve_relay()
     mix(1)
-    lax.fori_loop(0, hop, stage_a, 0)
+    backwards(stage_a, hop)
     l_finish(3)
     l_ready(2)
     mix(2)
-    lax.fori_loop(0, hop, stage_b, 0)
+    backwards(stage_b, hop)
     l_ready(3)
     mix(3)
-    lag = 2
-    for k in range(hop, last + 1 + 2 * lag):
-        if k < last:
-            stage_a(k, 0)
-        elif k == last:
-            antipode(functools.partial(one_a, last))
-        if k == hop + 1:
-            lax.fori_loop(0, hop, stage_c, 0)
-        kb = k - lag
-        if hop <= kb < last:
-            stage_b(kb, 0)
-        elif kb == last:
-            antipode(functools.partial(one_b, last))
-        kc = k - 2 * lag
-        if hop <= kc < last:
-            stage_c(kc, 0)
+    backwards(stage_c, hop)
+    antipode(functools.partial(one_a, last))
+    far(stage_a)
+    antipode(functools.partial(one_b, last))
+    far(stage_b)
     antipode(lambda kind: f_wait(kind, last).wait_recv())
     d2d(zhalf, 2 * last).start()
+    far(stage_c)
 
     def other(zz, k):
         ref = units.at[pl.ds((zz * 2 + 1 - c) * per, per)]
@@ -450,8 +455,9 @@
 
     lax.fori_loop(0, nv, last_mul, 0)
 
-    far5.wait_send()
-    far4.wait_send()
+    for b in range(BUNDLES):
+        for cp in bundle(b):
+            cp.wait_send()
     for g in range(parts):
         for cp in (*l_own(g), l_fwd(g), l_pair(0, g, c), l_pair(1, g, c), l_pair(2, g, c)):
             cp.wait_send()
@@ -508,13 +514,14 @@
             pl.BlockSpec(memory_space=SMEM),
             pl.BlockSpec(memory_space=SMEM),
             pl.BlockSpec(memory_space=SMEM),
-            pl.BlockSpec(memory_space=VMEM),
+            pl.BlockSpec(memory_space=pl.ANY),
             pl.BlockSpec(memory_space=pl.ANY),
             pl.BlockSpec(memory_space=VMEM),
             pl.BlockSpec(memory_space=VMEM),
         ],
         out_specs=pl.BlockSpec(memory_space=VMEM),
         scratch_shapes=[
+            VMEM((pool, tile, width), bf16),
             VMEM((n * nc * per, tile, LANES), bf16),
             VMEM((half, 5, tile, LANES), bf16),
             VMEM((half, 4, tile, LANES), bf16),
@@ -527,8 +534,9 @@
             VMEM((width, tiles * tile), bf16),
             VMEM((slab, states * width, 2 * LANES), bf16),
             DMA,
+            DMA,
             DMA((half,)), DMA((half,)), DMA((half,)), DMA((half,)),
-            DMA((2,)), DMA((2,)),
+            DMA((2, BUNDLES)), DMA((2, BUNDLES)),
             DMA((2, 2, half)), DMA((2, 2, half)),
             DMA((2, half)), DMA((2, half)),
             DMA((n,)), DMA((n,)),

time: 112 us -> 106 us (0.946)
  Pallas kernels: 109 us -> 102 us
    pallas_call x1, Pallas kernels: 107 us -> 101 us  [on_device(): pl.pallas_call(functools.partial(main_kernel, (n, nx, cap, thirds, bond))...]
where the time goes in v3:
time: 106 us
  Pallas kernels  102 us (96%)
  local copies, waits for them, and re-layouts  2.36 us (2%)
    pallas_call x1, Pallas kernels, on_device(): pl.pallas_call(functools.partial(main_kernel, (n, nx, cap, thirds, bond))...  101 us
    unnamed x1, local copies, waits for them, and re-layouts  2.36 us

profile of v3, /device:TPU:33, one launch (start us, length us, event | category | flops | bytes accessed | tf_op | source)
XLA Modules:
  0.0 105.5 jit_solution(6650051968554780719)
XLA Ops:
  0.7 1.6 %plan.1 = (s32[32,8]{1,0:T(8,128)}, s32[1,192]{1,0:T(1,128)}) custom-call(s32[32,192]{1,0:T(8,128)} %map_ref.1), custom_call_target="tpu_custom_call" | custom-call | tf_op jit(solution)/shard_map/plan/pallas_call | solution.py:502
  2.3 100.9 %exchange_and_contract.1 = f32[4,192,384]{2,1,0:T(8,128)} custom-call(s32[32,8]{1,0:T(8,128)} %get-tuple-element.7.src_ref, s32[1,192]{1,0:T(1,128)} %get-tuple-element.8.idx_ref, s32[1]{0:T(128)S(6)} %copy.10.kept_ref, f32[2]{0:T(128)} %fields_ref.1, bf16[192,8,384]{2,1,0:T(8,128)(2,1)} %pool_ref.1, bf16[4,384,384]{2,1,0:T(8,128)(2,1)} %bitcast.10, ...), custom_call_target="tpu_custom_call" | custom-call | tf_op jit(solution)/shard_map/exchange_and_contract/pallas_call | solution.py:509
  103.1 2.4 %copy.11 = f32[4,1,384,192]{2,3,1,0:T(8,128)} copy(f32[4,1,384,192]{2,3,1,0:T(8,128)} %bitcast.9) | data formatting | bytes 2359296

commit v4 on v3

--- a/solution.py
+++ b/solution.py
@@ -16,7 +16,7 @@
 BUNDLES = 2
 
 
-def plan_kernel(pool, cap, thirds, sectors, map_ref, src_ref, idx_ref):
+def find_tiles(pool, cap, thirds, map_ref, src_ref, idx_ref):
     tiles = map_ref.shape[1]
     row = lax.axis_index("env")
     me = row * lax.axis_size("col") + lax.axis_index("col")
@@ -35,19 +35,19 @@
     for r in range(cap):
         slot = jnp.sum(jnp.where(mine & (rank == float(r)), localf, 0.0), axis=1, keepdims=True)
         found = jnp.where(lane == r, slot, found)
-    src_ref[...] = found.astype(jnp.int32)
+    src_ref[...] = jnp.clip(found.astype(jnp.int32), 0, pool - 1)
     own = map_ref[pl.ds(row, 1), :].astype(jnp.float32)
     owner = jnp.floor((own + 0.5) * (1.0 / pool))
     same = lax.broadcasted_iota(jnp.int32, (tiles, tiles), 0) == lax.broadcasted_iota(jnp.int32, (tiles, tiles), 1)
     column = jnp.sum(jnp.where(same, jnp.broadcast_to(owner, (tiles, tiles)), 0.0), axis=1, keepdims=True)
     order = jnp.sum(jnp.where((column == owner) & before, 1.0, 0.0), axis=0, keepdims=True)
-    idx_ref[...] = (owner * float(cap * thirds) + order * float(thirds)).astype(jnp.int32)
+    idx_ref[0:1, 0:tiles] = (owner * float(cap * thirds) + order * float(thirds)).astype(jnp.int32)
 
 
 def main_kernel(
-    dims, src_ref, idx_ref, kept_ref, fields_ref, pool_ref, left_ref, mpo_ref, mask_ref, out_ref,
-    held_ref, units, sent5, sent4, relay5, relay4, lefts, kron, mixed, block, flipped, second,
-    load_sem, pool_sem, near5_s, near5_r, near4_s, near4_r, bund_s, bund_r, x_s, x_r, f_s, f_r, d_s, d_r,
+    dims, kept_ref, fields_ref, map_ref, pool_ref, left_ref, mpo_ref, mask_ref, out_ref,
+    src_v, idx_v, src_ref, idx_ref, held_ref, units, sent5, sent4, relay5, relay4, lefts, kron, mixed, block, flipped, second,
+    load_sem, pool_sem, table_sem, near5_s, near5_r, near4_s, near4_r, bund_s, bund_r, x_s, x_r, f_s, f_r, d_s, d_r,
     ln_s, ln_r, lf_s, lf_r, lp_s, lp_r,
 ):
     n, nx, cap, thirds, bond = dims
@@ -93,9 +93,18 @@
     pl.semaphore_signal(barrier, inc=1, device_id={"mpo": at_x(-1)}, device_id_type=MESH)
     pl.semaphore_signal(barrier, inc=1, device_id={"col": 1 - c}, device_id_type=MESH)
 
+    find_tiles(held_ref.shape[0], cap, thirds, map_ref, src_v, idx_v)
+    tables = [
+        pltpu.make_async_copy(src_v, src_ref, table_sem.at[0]),
+        pltpu.make_async_copy(idx_v, idx_ref, table_sem.at[1]),
+    ]
+    for cp in tables:
+        cp.start()
+
     def unit(t, u):
         r, h = u // thirds, lax.rem(u, thirds)
-        return held_ref[src_ref[t, r], :, pl.ds(pl.multiple_of(h * LANES, LANES), LANES)]
+        at = jnp.clip(src_ref[t, r], 0, held_ref.shape[0] - 1)
+        return held_ref[at, :, pl.ds(pl.multiple_of(h * LANES, LANES), LANES)]
 
     u5, u4 = start5(x), start4(x)
 
@@ -108,6 +117,8 @@
             sent4[k, i] = unit(t4, u4 + i)
         return 0
 
+    for cp in tables:
+        cp.wait()
     fetch.wait()
     lax.fori_loop(0, half, pick, 0)
 
@@ -295,12 +306,6 @@
             rcopy(ref, ref, x_s.at[1, kind, k], x_r.at[1, 1 - kind, k], {"mpo": at_x(-1)}),
         )
 
-    def x_wait(side, kind, k):
-        zz = at_z(-sgn * (k + 1)) if kind == 0 else at_z(sgn * (k + 1))
-        p = at_x(-1) if side == 0 else at_x(1)
-        ref = slot(zz, start4(p), 4) if kind == 0 else slot(zz, start5(p), 5)
-        return rcopy(ref, ref, x_s.at[side, kind, k], x_r.at[side, kind, k], {"mpo": at_x(1)})
-
     def f_send(kind, k):
         zz = at_z(-sgn * (k + 1)) if kind == 0 else at_z(sgn * (k + 1))
         p = at_x(-fdir)
@@ -333,15 +338,35 @@
     kinds = (0, 1)
     last = half - 1
 
+    def part(kind, k, off):
+        zz = at_z(-sgn * (k + 1)) if kind == 0 else at_z(sgn * (k + 1))
+        p = at_x(off)
+        five = (kind == 0) == (isinstance(off, int) and off % 2 == 0)
+        ref = slot(zz, start5(p), 5) if five else slot(zz, start4(p), 4)
+        at = 2 * last if isinstance(k, int) and k == last else 2 * k + kind
+        return rcopy(ref, ref, d_s.at[at], d_r.at[at], pside)
+
     def one_a(k, kind):
         z_wait(kind, k).wait_recv()
         for cp in x_send(kind, k):
             cp.start()
+        part(kind, k, 0).start()
+
+    def x_side(kind, k, side, off):
+        zz = at_z(-sgn * (k + 1)) if kind == 0 else at_z(sgn * (k + 1))
+        ref = slot(zz, start4(at_x(off)), 4) if kind == 0 else slot(zz, start5(at_x(off)), 5)
+        return rcopy(ref, ref, x_s.at[side, kind, k], x_r.at[side, kind, k], pside)
 
     def one_b(k, kind):
-        x_wait(0, kind, k).wait_recv()
-        x_wait(1, kind, k).wait_recv()
+        x_side(kind, k, c, -fdir).wait_recv()
         f_send(kind, k).start()
+        part(kind, k, -fdir).start()
+
+    def one_c(k, kind):
+        x_side(kind, k, 1 - c, fdir).wait_recv()
+        part(kind, k, fdir).start()
+        f_wait(kind, k).wait_recv()
+        part(kind, k, 2).start()
 
     def stage_a(k, _):
         for kind in kinds:
@@ -359,8 +384,7 @@
 
     def stage_c(k, _):
         for kind in kinds:
-            f_wait(kind, k).wait_recv()
-            to_other(kind, k).start()
+            one_c(k, kind)
         return 0
 
     def backwards(stage, top):
@@ -394,8 +418,7 @@
     far(stage_a)
     antipode(functools.partial(one_b, last))
     far(stage_b)
-    antipode(lambda kind: f_wait(kind, last).wait_recv())
-    d2d(zhalf, 2 * last).start()
+    antipode(functools.partial(one_c, last))
     far(stage_c)
 
     def other(zz, k):
@@ -416,7 +439,7 @@
     masks = [jnp.where(lane + h * LANES < kept_ref[0], 1.0, 0.0).astype(jnp.bfloat16) for h in range(thirds)]
 
     def place(j, _):
-        i0, i1 = idx_ref[0, 2 * j], idx_ref[0, 2 * j + 1]
+        i0, i1 = (jnp.clip(idx_ref[0, 2 * j + e], 0, units.shape[0] - thirds) for e in (0, 1))
         for h in range(thirds):
             two = jnp.concatenate([units[i0 + h], units[i1 + h]], axis=0)
             block[pl.ds(pl.multiple_of(j * ROWS, ROWS), ROWS), h * LANES : (h + 1) * LANES] = two * masks[h]
@@ -453,7 +476,8 @@
 
         return 0
 
-    lax.fori_loop(0, nv, last_mul, 0)
+    for v in range(nv):
+        last_mul(v, 0)
 
     for b in range(BUNDLES):
         for cp in bundle(b):
@@ -499,11 +523,6 @@
     half, hop = n // 2, n // 4
     bf16 = jnp.bfloat16
 
-    src, idx = pl.pallas_call(
-        functools.partial(plan_kernel, pool, cap, thirds, sectors),
-        out_shape=(jax.ShapeDtypeStruct((sectors, 8), jnp.int32), jax.ShapeDtypeStruct((1, tiles), jnp.int32)),
-        name="plan",
-    )(owner_map)
     mpo_rows = jnp.transpose(mpo_tensor, (0, 2, 3, 1)).reshape(bond * states * states, bond)
 
     out = pl.pallas_call(
@@ -512,8 +531,7 @@
         in_specs=[
             pl.BlockSpec(memory_space=SMEM),
             pl.BlockSpec(memory_space=SMEM),
-            pl.BlockSpec(memory_space=SMEM),
-            pl.BlockSpec(memory_space=SMEM),
+            pl.BlockSpec(memory_space=VMEM),
             pl.BlockSpec(memory_space=pl.ANY),
             pl.BlockSpec(memory_space=pl.ANY),
             pl.BlockSpec(memory_space=VMEM),
@@ -521,6 +539,10 @@
         ],
         out_specs=pl.BlockSpec(memory_space=VMEM),
         scratch_shapes=[
+            VMEM((sectors, LANES), jnp.int32),
+            VMEM((tile, 2 * LANES), jnp.int32),
+            SMEM((sectors, LANES), jnp.int32),
+            SMEM((tile, 2 * LANES), jnp.int32),
             VMEM((pool, tile, width), bf16),
             VMEM((n * nc * per, tile, LANES), bf16),
             VMEM((half, 5, tile, LANES), bf16),
@@ -535,6 +557,7 @@
             VMEM((slab, states * width, 2 * LANES), bf16),
             DMA,
             DMA,
+            DMA((2,)),
             DMA((half,)), DMA((half,)), DMA((half,)), DMA((half,)),
             DMA((2, BUNDLES)), DMA((2, BUNDLES)),
             DMA((2, 2, half)), DMA((2, 2, half)),
@@ -544,7 +567,7 @@
         ],
         compiler_params=pltpu.CompilerParams(collective_id=0, has_side_effects=True, vmem_limit_bytes=56 * 2**20),
         name="exchange_and_contract",
-    )(src, idx, kept, fields, held, left_env[:, 0], mpo_rows, mpo_mask)
+    )(kept, fields, owner_map, held, left_env[:, 0], mpo_rows, mpo_mask)
     return jnp.swapaxes(out, 1, 2)[:, None]
 
 

time: 106 us -> 107 us (level)
  Pallas kernels: 102 us -> 104 us
    pallas_call x1, Pallas kernels: 101 us -> 104 us  [on_device(): pl.pallas_call(functools.partial(main_kernel, (n, nx, cap, thirds, bond))...]
    pallas_call x1 -> x0, Pallas kernels: 1.61 us -> none  [on_device(): pl.pallas_call(functools.partial(plan_kernel, pool, cap, thirds, sectors)...]
where the time goes in v4:
time: 107 us
  Pallas kernels  104 us (97%)
  local copies, waits for them, and re-layouts  2.36 us (2%)
    pallas_call x1, Pallas kernels, on_device(): pl.pallas_call(functools.partial(main_kernel, (n, nx, cap, thirds, bond))...  104 us
    unnamed x1, local copies, waits for them, and re-layouts  2.36 us

profile of v4, /device:TPU:33, one launch (start us, length us, event | category | flops | bytes accessed | tf_op | source)
XLA Modules:
  0.0 106.5 jit_solution(15113799562189346795)
XLA Ops:
  0.7 103.5 %exchange_and_contract.1 = f32[4,192,384]{2,1,0:T(8,128)} custom-call(s32[1]{0:T(128)S(6)} %copy.10.kept_ref, f32[2]{0:T(128)} %fields_ref.1, s32[32,192]{1,0:T(8,128)} %map_ref.1, bf16[192,8,384]{2,1,0:T(8,128)(2,1)} %pool_ref.1, bf16[4,384,384]{2,1,0:T(8,128)(2,1)} %bitcast.10, f32[224,14]{1,0:T(8,128)} %bitcast.11, s32[14,14]{1,0:T(8,128)} %mask_ref.1), custom_call_target="tpu_custom_call" | custom-call | tf_op jit(solution)/shard_map/exchange_and_contract/pallas_call | solution.py:528
  104.2 2.4 %copy.11 = f32[4,1,384,192]{2,3,1,0:T(8,128)} copy(f32[4,1,384,192]{2,3,1,0:T(8,128)} %bitcast.9) | data formatting | bytes 2359296

commit v5 on v4

--- a/solution.py
+++ b/solution.py
@@ -120,14 +120,7 @@
     for cp in tables:
         cp.wait()
     fetch.wait()
-    lax.fori_loop(0, half, pick, 0)
-
-    def own(u, _):
-        units[(z * 2 + c) * per + u] = unit(z, u)
-        return 0
-
-    lax.fori_loop(0, per, own, 0)
-
+    lax.fori_loop(hop, half, pick, 0)
     load.wait()
     pl.semaphore_wait(barrier, 2 * hop + 3)
 
@@ -178,9 +171,6 @@
         for k in range(3):
             l_pair(k, g, 1 - c).wait_recv()
 
-    l_start(0)
-    l_start(1)
-
     step = hop // BUNDLES
 
     def bundle(b):
@@ -194,6 +184,9 @@
         for cp in bundle(b):
             cp.start()
 
+    l_start(0)
+    l_start(1)
+
     def near_copies(k):
         a = rcopy(sent5.at[k], slot(z, u5, 5), near5_s.at[k], near5_r.at[k], {"env": at_z(sgn * (k + 1))})
         b = rcopy(sent4.at[k], slot(z, u4, 4), near4_s.at[k], near4_r.at[k], {"env": at_z(-sgn * (k + 1))})
@@ -205,7 +198,14 @@
         b.start()
         return 0
 
+    lax.fori_loop(0, hop, pick, 0)
     lax.fori_loop(0, hop, near, 0)
+
+    def own(u, _):
+        units[(z * 2 + c) * per + u] = unit(z, u)
+        return 0
+
+    lax.fori_loop(0, per, own, 0)
 
     def d2d(zz, k):
         return rcopy(slot(zz, 0, per), slot(zz, 0, per), d_s.at[k], d_r.at[k], {"col": 1 - c})
@@ -400,12 +400,12 @@
     l_finish(1)
     l_ready(0)
     mix(0)
-    for b in range(BUNDLES - 1, -1, -1):
-        serve_relay(b)
     l_serve(3)
     l_finish(2)
     l_ready(1)
     mix(1)
+    for b in range(BUNDLES - 1, -1, -1):
+        serve_relay(b)
     backwards(stage_a, hop)
     l_finish(3)
     l_ready(2)

time: 107 us -> 106 us (level)
  no operation moved by 1% of the time
where the time goes in v5:
time: 106 us
  Pallas kernels  103 us (97%)
  local copies, waits for them, and re-layouts  2.36 us (2%)
    pallas_call x1, Pallas kernels, on_device(): pl.pallas_call(functools.partial(main_kernel, (n, nx, cap, thirds, bond))...  103 us
    unnamed x1, local copies, waits for them, and re-layouts  2.36 us

profile of v5, /device:TPU:33, one launch (start us, length us, event | category | flops | bytes accessed | tf_op | source)
XLA Modules:
  0.0 106.1 jit_solution(11772755406108602778)
XLA Ops:
  0.7 103.0 %exchange_and_contract.1 = f32[4,192,384]{2,1,0:T(8,128)} custom-call(s32[1]{0:T(128)S(6)} %copy.10.kept_ref, f32[2]{0:T(128)} %fields_ref.1, s32[32,192]{1,0:T(8,128)} %map_ref.1, bf16[192,8,384]{2,1,0:T(8,128)(2,1)} %pool_ref.1, bf16[4,384,384]{2,1,0:T(8,128)(2,1)} %bitcast.10, f32[224,14]{1,0:T(8,128)} %bitcast.11, s32[14,14]{1,0:T(8,128)} %mask_ref.1), custom_call_target="tpu_custom_call" | custom-call | tf_op jit(solution)/shard_map/exchange_and_contract/pallas_call | solution.py:528
  103.7 2.4 %copy.11 = f32[4,1,384,192]{2,3,1,0:T(8,128)} copy(f32[4,1,384,192]{2,3,1,0:T(8,128)} %bitcast.9) | data formatting | bytes 2359296
